TPU v7x, 32 devices: a whole 2x2x4 slice. The times are simulated.
32 devices in a mesh: seq: 8 (over z, core), batch: 4 (over y, x).
Axes of the slice: x: 2, y: 2, z: 4, core: 2. Of those that a mesh axis runs over, the one named last changes fastest.
Arguments:
- tokens: bfloat16 [4, 2048, 1152], P('batch', 'seq'), may hold values from -6 to 6
- long_skip: bfloat16 [4, 2048, 1152], P('batch', 'seq'), may hold values from -6 to 6
- lengths: int32 [4, 4], P('batch'), may hold values from 0 to 1026, as said below
- skip_weight: bfloat16 [2304, 1152], replicated, may hold values from -0.125 to 0.125
- skip_bias: bfloat16 [1152], replicated, may hold values from -3 to 3
- attention_gain: bfloat16 [1152], replicated, may hold values from 0.099609375 to 1.8984375
- attention_shift: bfloat16 [1152], replicated, may hold values from -3 to 3
- qkv_weight: bfloat16 [1152, 3456], replicated, may hold values from -0.1875 to 0.1875
- out_weight: bfloat16 [1152, 1152], replicated, may hold values from -2 to 2
- out_bias: bfloat16 [1152], replicated, may hold values from -3 to 3
- mlp_gain: bfloat16 [1152], replicated, may hold values from 0.099609375 to 1.8984375
- mlp_shift: bfloat16 [1152], replicated, may hold values from -3 to 3
- hidden_weight: bfloat16 [1152, 4608], replicated, may hold values from -0.1875 to 0.1875
- hidden_bias: bfloat16 [4608], replicated, may hold values from -3 to 3
- down_weight: bfloat16 [4608, 1152], replicated, may hold values from -0.09375 to 0.09375
- down_bias: bfloat16 [1152], replicated, may hold values from -3 to 3
- cotangent: bfloat16 [4, 2048, 1152], P('batch', 'seq'), may hold values from -6 to 6
Outputs:
- output: bfloat16 [4, 2048, 1152], P('batch', 'seq')
- grad_tokens: float32 [4, 2048, 1152], P('batch', 'seq')
- grad_long_skip: float32 [4, 2048, 1152], P('batch', 'seq')
- grad_skip_weight: float32 [2304, 1152], P('batch', 'seq')
- grad_skip_bias: float32 [1152], replicated
- grad_attention_gain: float32 [1152], replicated
- grad_attention_shift: float32 [1152], replicated
- grad_qkv_weight: float32 [1152, 3456], P('batch', 'seq')
- grad_out_weight: float32 [1152, 1152], P('batch', 'seq')
- grad_out_bias: float32 [1152], replicated
- grad_mlp_gain: float32 [1152], replicated
- grad_mlp_shift: float32 [1152], replicated
- grad_hidden_weight: float32 [1152, 4608], P('batch', 'seq')
- grad_hidden_bias: float32 [4608], replicated
- grad_down_weight: float32 [4608, 1152], P('batch', 'seq')
- grad_down_bias: float32 [1152], replicated
Inputs may be any that keep to these rules, and one draw needn't show every extreme that they name: Row g lists the lengths of group g's items in the order in which they lie along the group's 2048 positions. Each entry is 258, 1026 or 0, every row has one or more entries 1026, zeros stand only after the last nonzero entry, and the row's total leaves fewer than 258 positions of padding at the end.
All inputs are finite; a program needn't handle non-finite values.
Results may differ from a plain program's by a relative error of at most 0.013.
Values may be sent and summed in bfloat16 or wider, within the bound.
A program may use at most 256 MiB of HBM per device.

v0:
```python
import math
import jax
import jax.numpy as jnp
from jax import lax
from jax.sharding import PartitionSpec as P

HD = 72
norm_eps = 1e-05


def product(left, right):
    return jnp.dot(left, right, preferred_element_type=jnp.float32)


def contract_rows(left, right):
    return lax.dot_general(
        left, right, (((0,), (0,)), ((), ())), preferred_element_type=jnp.float32
    )


def times_transposed(left, right):
    return lax.dot_general(
        left, right, (((1,), (1,)), ((), ())), preferred_element_type=jnp.float32
    )


def column_sums(values):
    return jnp.sum(values.astype(jnp.float32), axis=0)


def layer_norm(inputs, gain, shift):
    mean_row = jnp.mean(inputs, axis=-1, keepdims=True)
    centred = inputs - mean_row
    spread = jnp.mean(centred * centred, axis=-1, keepdims=True)
    return centred * lax.rsqrt(spread + norm_eps) * gain + shift


def exact_gelu(inputs):
    return jax.nn.gelu(inputs, approximate=False)


def segments(row_lengths, group_len):
    ends = jnp.cumsum(row_lengths)
    places = jnp.arange(group_len, dtype=jnp.int32)
    return jnp.sum((places[:, None] >= ends[None, :]).astype(jnp.int32), axis=1)


def score_block(query_block, key_heads, seg_block, segment):
    raw = jnp.einsum("bhd,khd->hbk", query_block, key_heads, preferred_element_type=jnp.float32)
    scores = raw * (1.0 / math.sqrt(HD))
    allowed = (seg_block[:, None] == segment[None, :])[None]
    return jnp.where(allowed, scores, -jnp.inf)


def attend_forward(query_heads, key_flat, value_flat, segment):
    length, head_cols = query_heads.shape
    head_count = head_cols // HD
    block_rows = min(512, length)
    block_count = length // block_rows
    key_heads = key_flat.reshape(length, head_count, HD)
    value_heads = value_flat.reshape(length, head_count, HD)

    def one_block(pieces):
        query_block, seg_block = pieces
        scores = score_block(query_block, key_heads, seg_block, segment)
        row_max = jnp.max(scores, axis=2, keepdims=True)
        log_total = row_max + jnp.log(jnp.sum(jnp.exp(scores - row_max), axis=2, keepdims=True))
        probs_low = jnp.exp(scores - log_total).astype(jnp.bfloat16)
        context = jnp.einsum(
            "hbk,khd->bhd", probs_low, value_heads, preferred_element_type=jnp.float32
        )
        return (context.astype(jnp.bfloat16).reshape(block_rows, head_cols), log_total)

    context, log_total = lax.map(
        one_block,
        (
            query_heads.reshape(block_count, block_rows, head_count, HD),
            segment.reshape(block_count, block_rows),
        ),
    )
    return (context.reshape(length, head_cols), log_total)


def attend_backward(query_heads, key_flat, value_flat, segment, grad_context, log_total):
    length, head_cols = query_heads.shape
    head_count = head_cols // HD
    block_rows = min(512, length)
    block_count = length // block_rows
    score_scale = 1.0 / math.sqrt(HD)
    key_heads = key_flat.reshape(length, head_count, HD)
    value_heads = value_flat.reshape(length, head_count, HD)

    def one_block(totals, pieces):
        grad_keys, grad_values = totals
        query_block, seg_block, grad_block, total_block = pieces
        scores = score_block(query_block, key_heads, seg_block, segment)
        prob_full = jnp.exp(scores - total_block)
        probs_low = prob_full.astype(jnp.bfloat16)
        grad_values = grad_values + jnp.einsum(
            "hbk,bhd->khd", probs_low, grad_block, preferred_element_type=jnp.float32
        )
        grad_probs = jnp.einsum(
            "bhd,khd->hbk", grad_block, value_heads, preferred_element_type=jnp.float32
        )
        row_delta = jnp.sum(prob_full * grad_probs, axis=2, keepdims=True)
        grad_scores = (prob_full * (grad_probs - row_delta)).astype(jnp.bfloat16)
        grad_query = (
            jnp.einsum("hbk,khd->bhd", grad_scores, key_heads, preferred_element_type=jnp.float32)
            * score_scale
        )
        grad_keys = grad_keys + jnp.einsum(
            "hbk,bhd->khd", grad_scores, query_block, preferred_element_type=jnp.float32
        )
        return (
            (grad_keys, grad_values),
            grad_query.astype(jnp.bfloat16).reshape(block_rows, head_cols),
        )

    empty_sum = jnp.zeros((length, head_count, HD), jnp.float32)
    (grad_keys, grad_values), grad_query = lax.scan(
        one_block,
        (empty_sum, empty_sum),
        (
            query_heads.reshape(block_count, block_rows, head_count, HD),
            segment.reshape(block_count, block_rows),
            grad_context.reshape(block_count, block_rows, head_count, HD),
            log_total,
        ),
    )
    grad_keys = (grad_keys * score_scale).astype(jnp.bfloat16).reshape(length, head_cols)
    grad_values = grad_values.astype(jnp.bfloat16).reshape(length, head_cols)
    return (grad_query.reshape(length, head_cols), grad_keys, grad_values)


def seq_gathered_grad(left, right):
    left_all = lax.all_gather(left, "seq", axis=0, tiled=True)
    right_cols = lax.all_to_all(right, "seq", split_axis=1, concat_axis=0, tiled=True)
    partial = contract_rows(left_all, right_cols).astype(jnp.bfloat16)
    summed = lax.psum_scatter(partial, "batch", scatter_dimension=0, tiled=True)
    return summed.astype(jnp.float32)


def batch_gathered_grad(left, right):
    left_rows = lax.all_to_all(left, "batch", split_axis=1, concat_axis=0, tiled=True)
    right_all = lax.all_gather(right, "batch", axis=0, tiled=True)
    partial = contract_rows(left_rows, right_all).astype(jnp.bfloat16)
    summed = lax.psum_scatter(partial, "seq", scatter_dimension=1, tiled=True)
    return summed.astype(jnp.float32)


def qkv_grad_from_heads(left, grad_heads):
    seq_count = lax.axis_size("seq")
    me = lax.axis_index("seq")
    piece = grad_heads.shape[1] // 3
    left_all = lax.all_gather(left, "seq", axis=0, tiled=True)
    partial = contract_rows(left_all, grad_heads).astype(jnp.bfloat16)
    summed = lax.psum_scatter(partial, "batch", scatter_dimension=0, tiled=True)
    summed = summed.astype(jnp.float32)
    inverse = pow(3, -1, seq_count)
    slots = []
    for slot in range(3):
        target = (me - slot) * inverse % seq_count
        chunk = (3 * target + slot) // seq_count
        sent = lax.dynamic_slice_in_dim(summed, chunk * piece, piece, axis=1)
        pairs = []
        for source in range(seq_count):
            pairs.append((source, (source - slot) * inverse % seq_count))
        slots.append(lax.ppermute(sent, "seq", pairs))
    return jnp.concatenate(slots, axis=1)


GRAD_PLAN = {"skip": "batch", "qkv": "seq", "out": "batch", "hidden": "seq", "down": "batch"}


def weight_grad(name, left, right):
    if GRAD_PLAN[name] == "seq":
        return seq_gathered_grad(left, right)
    return batch_gathered_grad(left, right)


def on_device(
    tokens,
    long_skip,
    lengths,
    skip_weight,
    skip_bias,
    attention_gain,
    attention_shift,
    qkv_weight,
    out_weight,
    out_bias,
    mlp_gain,
    mlp_shift,
    hidden_weight,
    hidden_bias,
    down_weight,
    down_bias,
    cotangent,
):
    local_rows = tokens.shape[1]
    feature_count = tokens.shape[2]
    group_len = local_rows * lax.axis_size("seq")
    joined = jnp.concatenate([tokens[0], long_skip[0]], axis=1)
    mixed = product(joined, skip_weight) + skip_bias.astype(jnp.float32)
    normed_full, first_pull = jax.vjp(
        layer_norm, mixed, attention_gain.astype(jnp.float32), attention_shift.astype(jnp.float32)
    )
    normed_one = normed_full.astype(jnp.bfloat16)
    packed = product(normed_one, qkv_weight).astype(jnp.bfloat16)
    seq_count = lax.axis_size("seq")
    packed_heads = lax.all_to_all(
        packed.reshape(local_rows, 3, seq_count, feature_count // seq_count),
        "seq",
        split_axis=2,
        concat_axis=0,
        tiled=True,
    ).reshape(group_len, 3, feature_count // seq_count)
    query_heads = packed_heads[:, 0]
    key_heads = packed_heads[:, 1]
    value_heads = packed_heads[:, 2]
    segment = segments(lengths[0], group_len)
    context_heads, log_total = attend_forward(query_heads, key_heads, value_heads, segment)
    context_tok = lax.all_to_all(context_heads, "seq", split_axis=0, concat_axis=1, tiled=True)
    middle = mixed + product(context_tok, out_weight) + out_bias.astype(jnp.float32)
    second_full, second_pull = jax.vjp(
        layer_norm, middle, mlp_gain.astype(jnp.float32), mlp_shift.astype(jnp.float32)
    )
    normed_two = second_full.astype(jnp.bfloat16)
    hidden_pre = product(normed_two, hidden_weight) + hidden_bias.astype(jnp.float32)
    act_full, gelu_pull = jax.vjp(exact_gelu, hidden_pre)
    hidden_act = act_full.astype(jnp.bfloat16)
    output = (middle + product(hidden_act, down_weight) + down_bias.astype(jnp.float32)).astype(
        jnp.bfloat16
    )
    grad_out_rows = cotangent[0]
    grad_down_weight = weight_grad("down", hidden_act, grad_out_rows)
    grad_down_bias = column_sums(grad_out_rows)
    grad_act = times_transposed(grad_out_rows, down_weight)
    grad_pre = gelu_pull(grad_act)[0].astype(jnp.bfloat16)
    grad_hidden_weight = weight_grad("hidden", normed_two, grad_pre)
    grad_hidden_bias = column_sums(grad_pre)
    grad_normed_two = times_transposed(grad_pre, hidden_weight)
    grad_middle_norm, grad_mlp_gain, grad_mlp_shift = second_pull(grad_normed_two)
    grad_middle = grad_out_rows.astype(jnp.float32) + grad_middle_norm
    grad_attended = grad_middle.astype(jnp.bfloat16)
    grad_out_bias = column_sums(grad_attended)
    grad_out_weight = weight_grad("out", context_tok, grad_attended)
    grad_context = times_transposed(grad_attended, out_weight).astype(jnp.bfloat16)
    grad_context_heads = lax.all_to_all(
        grad_context, "seq", split_axis=1, concat_axis=0, tiled=True
    )
    grad_query, grad_key, grad_value = attend_backward(
        query_heads, key_heads, value_heads, segment, grad_context_heads, log_total
    )
    grad_packed = jnp.concatenate(
        [
            lax.all_to_all(grad_query, "seq", split_axis=0, concat_axis=1, tiled=True),
            lax.all_to_all(grad_key, "seq", split_axis=0, concat_axis=1, tiled=True),
            lax.all_to_all(grad_value, "seq", split_axis=0, concat_axis=1, tiled=True),
        ],
        axis=1,
    )
    grad_qkv_weight = qkv_grad_from_heads(
        normed_one, jnp.concatenate([grad_query, grad_key, grad_value], axis=1)
    )
    grad_normed_one = times_transposed(grad_packed, qkv_weight)
    grad_mixed_norm, grad_attention_gain, grad_attention_shift = first_pull(grad_normed_one)
    grad_mixed = (grad_middle + grad_mixed_norm).astype(jnp.bfloat16)
    grad_skip_bias = column_sums(grad_mixed)
    grad_skip_weight = weight_grad("skip", joined, grad_mixed)
    grad_joined = times_transposed(grad_mixed, skip_weight)
    grad_tokens = grad_joined[:, :feature_count][None]
    grad_long_skip = grad_joined[:, feature_count:][None]
    summed_weights = (
        grad_skip_weight,
        grad_qkv_weight,
        grad_out_weight,
        grad_hidden_weight,
        grad_down_weight,
    )
    small_grads = (
        grad_skip_bias,
        grad_attention_gain,
        grad_attention_shift,
        grad_out_bias,
        grad_mlp_gain,
        grad_mlp_shift,
        grad_hidden_bias,
        grad_down_bias,
    )
    small_sizes = [piece.shape[0] for piece in small_grads]
    small_total = lax.psum(jnp.concatenate(small_grads), ("seq", "batch"))
    summed_small = []
    offset = 0
    for size in small_sizes:
        summed_small.append(small_total[offset : offset + size])
        offset += size
    return (
        output[None],
        grad_tokens,
        grad_long_skip,
        summed_weights[0],
        summed_small[0],
        summed_small[1],
        summed_small[2],
        summed_weights[1],
        summed_weights[2],
        summed_small[3],
        summed_small[4],
        summed_small[5],
        summed_weights[3],
        summed_small[6],
        summed_weights[4],
        summed_small[7],
    )


def solution(mesh):
    in_specs = (
        P("batch", "seq", None),
        P("batch", "seq", None),
        P("batch", None),
        P(),
        P(),
        P(),
        P(),
        P(),
        P(),
        P(),
        P(),
        P(),
        P(),
        P(),
        P(),
        P(),
        P("batch", "seq", None),
    )
    out_specs = (
        P("batch", "seq", None),
        P("batch", "seq", None),
        P("batch", "seq", None),
        P("batch", "seq"),
        P(),
        P(),
        P(),
        P("batch", "seq"),
        P("batch", "seq"),
        P(),
        P(),
        P(),
        P("batch", "seq"),
        P(),
        P("batch", "seq"),
        P(),
    )
    return jax.shard_map(
        on_device, mesh=mesh, in_specs=in_specs, out_specs=out_specs, check_vma=False
    )
```

profile of v0, /device:TPU:0, one launch (start us, length us, event | category | flops | bytes accessed | tf_op | source)
XLA Modules:
  0.0 722.0 jit_solution(6150779179004533748)
XLA Ops:
  16.0 7.2 %convolution_convert_fusion.1 = bf16[256,3456]{1,0:T(8,128)(2,1)} fusion(bf16[256,1152]{1,0:T(8,128)(2,1)S(1)} %add_convert_fusion.3, bf16[1152,3456]{1,0:T(8,128)(2,1)} %param.28), kind=kOutput, calls=%fused_computation.53 | convolution fusion | flops 2039316480 | bytes 10321920 | tf_op jit(solution)/shard_map/dot_general | solution.py:12
  29.9 6.6 all-to-all-start
  36.8 41.7 %all-to-all-done = bf16[256,3,8,144]{0,3,1,2:T(8,128)(2,1)} async-done(((bf16[256,3,8,144]{0,3,1,2:T(8,128)(2,1)}), bf16[256,3,8,144]{0,3,1,2:T(8,128)(2,1)}, u32[]{:S(2)}, u32[]{:S(2)}) %all-to-all-start) | async-done | bytes 1769504 | tf_op jit(solution)/shard_map/all_to_all | solution.py:211
  93.8 36.5 %while.27 = (s32[]{:T(128)}, bf16[4,512,144]{1,2,0:T(8,128)(2,1)}, f32[4,2,512,1]{2,1,3,0:T(2,128)S(1)}, s32[4,512]{1,0:T(4,128)S(1)}, s32[2048]{0:T(1024)S(1)},...) while((s32[]{:T(128)}, bf16[4,512,144]{1,2,0:T(8,128)(2,1)}, ...), condition=%wide.region_7.8_spmd, body=%wide.region_4.7_spmd.sunk | while | flops 628169728 | bytes 33536144 | solution.py:74
  142.0 20.8 %all-to-all-done.1 = bf16[8,256,144]{1,2,0:T(8,128)(2,1)} async-done(((bf16[8,256,144]{1,2,0:T(8,128)(2,1)}), bf16[8,256,144]{1,2,0:T(8,128)(2,1)}, u32[]{:S(2)}, u32[]{:S(2)}) %all-to-all-start.1) | async-done | bytes 589856 | tf_op jit(solution)/shard_map/all_to_all | solution.py:223
  167.6 17.2 %multiply_convert_fusion.1 = (bf16[256,4608]{1,0:T(8,128)(2,1)}, f32[256,4608]{1,0:T(8,128)}, f32[256,4608]{1,0:T(8,128)}) fusion(f32[4608]{0:T(1024)S(1)} %convert_element_type.134, bf16[256,1152]{1,0:T(8,128)(2,1)} %add_convert_fusion.2, bf16[1152,4608]{1,0:T(8,128)(2,1)} %param.33), kind=kOutput, calls=%fused_computation.57 | convolution fusion | flops 2795765760 | bytes 23021568 | tf_op jit(solution)/shard_map/dot_general | solution.py:12
  184.8 14.7 %convert_reduce_fusion = (f32[4608]{0:T(1024)}, bf16[256,4608]{1,0:T(8,128)(2,1)}) fusion(f32[256,4608]{1,0:T(8,128)} %get-tuple-element.290, f32[256,4608]{1,0:T(8,128)} %get-tuple-element.315, bf16[4608,1152]{1,0:T(8,128)(2,1)} %param.35, bf16[1,256,1152]{2,1,0:T(8,128)(2,1)S(1)} %copy-done.14), kind=kOutput, calls=%fused_computation.55 | convolution fusion | flops 2736778752 | bytes 23021568 | tf_op jit(solution)/shard_map/dot_general | solution.py:22
  199.5 8.7 %multiply_reduce_fusion.1 = (f32[1152]{0:T(1024)}, f32[256]{0:T(256)S(1)}, f32[1152]{0:T(1024)}, f32[256,1152]{1,0:T(8,128)S(1)}) fusion(f32[256,1152]{1,0:T(8,128)S(1)} %copy-done.7, f32[256]{0:T(256)S(1)} %fusion.69, f32[256]{0:T(256)S(1)} %broadcast_multiply_fusion, f32[1152]{0:T(1024)S(1)} %convert_element_type.131, ...), kind=kOutput, calls=%fused_computation.106 | convolution fusion | flops 2720265728 | bytes 15352320 | tf_op jit(solution)/shard_map/dot_general | solution.py:22
  220.7 15.9 %all-to-all-done.2 = bf16[256,8,144]{0,2,1:T(8,128)(2,1)S(1)} async-done(((bf16[256,8,144]{0,2,1:T(8,128)(2,1)}), bf16[256,8,144]{0,2,1:T(8,128)(2,1)S(1)}, u32[]{:S(2)}, u32[]{:S(2)}) %all-to-all-start.2) | async-done | bytes 589856 | tf_op jit(solution)/shard_map/all_to_all | solution.py:249
  239.0 87.2 %while.28 = (s32[]{:T(128)}, f32[2048,2,72]{0,2,1:T(8,128)S(1)}, f32[2048,2,72]{0,2,1:T(8,128)}, bf16[4,512,144]{1,2,0:T(8,128)(2,1)}, bf16[4,512,2,72]{1,3,2,0:...) while((s32[]{:T(128)}, f32[2048,2,72]{0,2,1:T(8,128)S(1)}, ...), condition=%wide.region_14.15_spmd.clone, body=%wide.region_12.14_spmd.clone.sunk | while | flops 1543781376 | bytes 136800560 | solution.py:120
  253.5 5.1 fusion.146
  275.3 5.2 fusion.146
  297.1 5.2 fusion.146
  318.9 5.2 fusion.146
  334.1 15.5 %all-to-all-done.5 = bf16[8,256,144]{1,2,0:T(8,128)(2,1)} async-done(((bf16[8,256,144]{1,2,0:T(8,128)(2,1)}), bf16[8,256,144]{1,2,0:T(8,128)(2,1)}, u32[]{:S(2)}, u32[]{:S(2)}) %all-to-all-start.5) | async-done | bytes 589856 | tf_op jit(solution)/shard_map/all_to_all | solution.py:259
  357.3 13.3 %all-to-all-done.4 = bf16[8,256,144]{1,2,0:T(8,128)(2,1)} async-done(((bf16[8,256,144]{1,2,0:T(8,128)(2,1)}), bf16[8,256,144]{1,2,0:T(8,128)(2,1)}, u32[]{:S(2)}, u32[]{:S(2)}) %all-to-all-start.4) | async-done | bytes 589856 | tf_op jit(solution)/shard_map/all_to_all | solution.py:258
  370.6 19.3 %all_to_all.180 = bf16[8,256,144]{1,2,0:T(8,128)(2,1)S(1)} all-to-all(bf16[8,256,144]{1,2,0:T(8,128)(2,1)S(1)} %copy.108), channel_id=1, replica_groups=mesh['seq'=8,'batch'=4] {'seq'}, dimensions={0} | all-to-all | bytes 1179648 | tf_op jit(solution)/shard_map/all_to_all | solution.py:257
  389.9 6.5 multiply_reduce_fusion.2
  399.8 6.0 convolution_convert_fusion.4
  411.6 9.8 %all-to-all-done.7 = bf16[256,4,288]{0,2,1:T(8,128)(2,1)S(1)} async-done(((bf16[256,4,288]{0,2,1:T(8,128)(2,1)}), bf16[256,4,288]{0,2,1:T(8,128)(2,1)S(1)}, u32[]{:S(2)}, u32[]{:S(2)}) %all-to-all-start.7) | async-done | bytes 589856 | tf_op jit(solution)/shard_map/all_to_all | solution.py:144
  425.9 4.7 convolution_convert_fusion.5
  430.9 34.5 %all-to-all-done.9 = bf16[256,4,1152]{2,0,1:T(8,128)(2,1)S(1)} async-done(((bf16[256,4,1152]{2,0,1:T(8,128)(2,1)}), bf16[256,4,1152]{2,0,1:T(8,128)(2,1)S(1)}, u32[]{:S(2)}, u32[]{:S(2)}) %all-to-all-start.9) | async-done | bytes 2359328 | tf_op jit(solution)/shard_map/all_to_all | solution.py:144
  465.5 6.5 convolution_convert_fusion
  482.2 10.3 %all-to-all-done.6 = bf16[256,4,576]{0,2,1:T(8,128)(2,1)S(1)} async-done(((bf16[256,4,576]{0,2,1:T(8,128)(2,1)}), bf16[256,4,576]{0,2,1:T(8,128)(2,1)S(1)}, u32[]{:S(2)}, u32[]{:S(2)}) %all-to-all-start.6) | async-done | bytes 1179680 | tf_op jit(solution)/shard_map/all_to_all | solution.py:144
  500.5 5.2 convolution_convert_fusion.3
  506.3 61.5 %all-to-all-done.8 = bf16[256,8,576]{0,2,1:T(8,128)(2,1)S(1)} async-done(((bf16[256,8,576]{0,2,1:T(8,128)(2,1)}), bf16[256,8,576]{0,2,1:T(8,128)(2,1)S(1)}, u32[]{:S(2)}, u32[]{:S(2)}) %all-to-all-start.8) | async-done | bytes 2359328 | tf_op jit(solution)/shard_map/all_to_all | solution.py:137
  569.6 8.2 %convolution_convert_fusion.2 = bf16[1152,576]{1,0:T(8,128)(2,1)} fusion(bf16[2048,1152]{1,0:T(8,128)(2,1)} %all-gather.13.cloned.1.call-done, bf16[2048,576]{0,1:T(8,128)(2,1)} %bitcast.219), kind=kOutput, calls=%fused_computation.71 | convolution fusion | flops 2718572544 | bytes 8404992 | tf_op jit(solution)/shard_map/dot_general | solution.py:16
  578.0 8.9 %fusion.47 = bf16[1,256,1152]{2,1,0:T(8,128)(2,1)} fusion(f32[256,1152]{1,0:T(8,128)S(1)} %copy-done.8, bf16[256,4608]{1,0:T(8,128)(2,1)} %get-tuple-element.289, bf16[4608,1152]{1,0:T(8,128)(2,1)} %param.35, f32[1152]{0:T(1024)S(1)} %convert_element_type.136), kind=kOutput, calls=%fused_computation.82 | convolution fusion | flops 2718793728 | bytes 14750208 | tf_op jit(solution)/shard_map/dot_general | solution.py:12
  587.0 38.9 %psum.7 = f32[12672]{0:T(1024)S(1)} all-reduce(f32[12672]{0:T(1024)S(1)} %constant_dynamic-update-slice_fusion), channel_id=1, replica_groups=mesh['seq'=8,'batch'=4] {'seq','batch'}, use_global_device_ids=true, to_apply=%region_26.27 | all-reduce | flops 12672 | bytes 101376 | tf_op jit(solution)/shard_map/psum | solution.py:292
  642.9 10.9 %collective-permute-done.2 = f32[288,144]{1,0:T(8,128)} collective-permute-done((f32[288,144]{1,0:T(8,128)}, f32[288,144]{1,0:T(8,128)}, u32[]{:S(2)}, u32[]{:S(2)}) %collective-permute-start.2) | collective-permute-done | bytes 165920 | tf_op jit(solution)/shard_map/ppermute | solution.py:168
  657.9 23.6 %reduce-scatter.6.cloned.1.call-done = bf16[576,144]{0,1:T(8,128)(2,1)} async-done(((bf16[576,1152]{0,1:T(8,128)(2,1)}), bf16[576,144]{0,1:T(8,128)(2,1)}) %reduce-scatter.6.cloned.1.call-update) | async-done | bytes 165904 | tf_op jit(solution)/shard_map/reduce_scatter | solution.py:147
  683.2 29.8 %reduce-scatter.12.cloned.1.call-done = bf16[288,576]{1,0:T(8,128)(2,1)} async-done(((bf16[1152,576]{1,0:T(8,128)(2,1)}), bf16[288,576]{1,0:T(8,128)(2,1)}) %reduce-scatter.12.cloned.1.call-update) | async-done | bytes 331792 | tf_op jit(solution)/shard_map/reduce_scatter | solution.py:139
  (320 shorter events, 239.0 us)
Async XLA Ops:
  7.2 155.6 %copy-start = (bf16[1152,1152]{1,0:T(8,128)(2,1)S(1)}, bf16[1152,1152]{1,0:T(8,128)(2,1)}, u32[]{:S(2)}) copy-start(bf16[1152,1152]{1,0:T(8,128)(2,1)} %param.29) | copy-start | bytes 7962628
  29.9 48.6 %all-to-all-start = ((bf16[256,3,8,144]{0,3,1,2:T(8,128)(2,1)}), bf16[256,3,8,144]{0,3,1,2:T(8,128)(2,1)}, u32[]{:S(2)}, u32[]{:S(2)}) async-start(bf16[256,3,8,144]{0,3,1,2:T(8,128)(2,1)} %copy.98), calls=%async_computation | async-start | bytes 3538944 | tf_op jit(solution)/shard_map/all_to_all | solution.py:211
  137.0 25.9 %all-to-all-start.1 = ((bf16[8,256,144]{1,2,0:T(8,128)(2,1)}), bf16[8,256,144]{1,2,0:T(8,128)(2,1)}, u32[]{:S(2)}, u32[]{:S(2)}) async-start(bf16[8,256,144]{1,2,0:T(8,128)(2,1)} %copy.102), calls=%async_computation.1 | async-start | bytes 1179648 | tf_op jit(solution)/shard_map/all_to_all | solution.py:223
  141.2 258.6 %all-gather.9.cloned.1.call-start = ((), (), s32[]{:S(2)}) async-start(), calls=%async_computation.17 | async-start | bytes 5308416 | tf_op jit(solution)/shard_map/all_gather | solution.py:155
  167.6 17.2 %copy-start.14 = (bf16[1,256,1152]{2,1,0:T(8,128)(2,1)S(1)}, bf16[1,256,1152]{2,1,0:T(8,128)(2,1)}, u32[]{:S(2)}) copy-start(bf16[1,256,1152]{2,1,0:T(8,128)(2,1)} %param.37) | copy-start | bytes 1769476
  216.4 20.2 %all-to-all-start.2 = ((bf16[256,8,144]{0,2,1:T(8,128)(2,1)}), bf16[256,8,144]{0,2,1:T(8,128)(2,1)S(1)}, u32[]{:S(2)}, u32[]{:S(2)}) async-start(bf16[256,8,144]{0,2,1:T(8,128)(2,1)} %bitcast.18), calls=%async_computation.2 | async-start | bytes 1179648 | tf_op jit(solution)/shard_map/all_to_all | solution.py:249
  220.0 206.0 %all-gather.11.cloned.1.call-start = ((), (), s32[]{:S(2)}) async-start(), calls=%async_computation.19 | async-start | bytes 2949120 | tf_op jit(solution)/shard_map/all_gather | solution.py:145
  328.6 26.1 %copy-start.13 = (bf16[4,512,144]{1,2,0:T(8,128)(2,1)S(1)}, bf16[4,512,144]{1,2,0:T(8,128)(2,1)}, u32[]{:S(2)}) copy-start(bf16[4,512,144]{1,2,0:T(8,128)(2,1)} %get-tuple-element.120) | copy-start | bytes 1769476
  328.6 21.1 %all-to-all-start.5 = ((bf16[8,256,144]{1,2,0:T(8,128)(2,1)}), bf16[8,256,144]{1,2,0:T(8,128)(2,1)}, u32[]{:S(2)}, u32[]{:S(2)}) async-start(bf16[8,256,144]{1,2,0:T(8,128)(2,1)} %copy.110), calls=%async_computation.5 | async-start | bytes 1179648 | tf_op jit(solution)/shard_map/all_to_all | solution.py:259
  333.0 24.2 %copy-start.19 = (bf16[2048,2,72]{0,2,1:T(8,128)(2,1)}, bf16[2048,2,72]{0,2,1:T(8,128)(2,1)S(1)}, u32[]{:S(2)}) copy-start(bf16[2048,2,72]{0,2,1:T(8,128)(2,1)S(1)} %multiply_convert_fusion.2) | copy-start | bytes 1769476
  334.1 55.8 %copy-start.10 = (f32[256,1152]{1,0:T(8,128)S(1)}, f32[256,1152]{1,0:T(8,128)}, u32[]{:S(2)}) copy-start(f32[256,1152]{1,0:T(8,128)} %copy-done.9) | copy-start | bytes 3538948
  334.1 55.8 %copy-start.29 = (f32[1152]{0:T(1024)S(1)}, f32[1152]{0:T(1024)}, u32[]{:S(2)}) copy-start(f32[1152]{0:T(1024)} %copy-done.28) | copy-start | bytes 13828
  334.1 55.8 %copy-start.33 = (f32[256]{0:T(256)S(1)}, f32[256]{0:T(256)}, u32[]{:S(2)}) copy-start(f32[256]{0:T(256)} %copy-done.32) | copy-start | bytes 3076
  334.1 55.8 %copy-start.38 = (f32[256]{0:T(256)S(1)}, f32[256]{0:T(256)}, u32[]{:S(2)}) copy-start(f32[256]{0:T(256)} %copy-done.37) | copy-start | bytes 3076
  349.7 20.9 %all-to-all-start.4 = ((bf16[8,256,144]{1,2,0:T(8,128)(2,1)}), bf16[8,256,144]{1,2,0:T(8,128)(2,1)}, u32[]{:S(2)}, u32[]{:S(2)}) async-start(bf16[8,256,144]{1,2,0:T(8,128)(2,1)} %copy.109), calls=%async_computation.4 | async-start | bytes 1179648 | tf_op jit(solution)/shard_map/all_to_all | solution.py:258
  353.9 77.1 %all-gather.15.cloned.1.call-start = ((), (), s32[]{:S(2)}) async-start(), calls=%async_computation.24 | async-start | bytes 2949120 | tf_op jit(solution)/shard_map/all_gather | solution.py:145
  354.6 145.9 %all-gather.7.cloned.1.call-start = ((), (), s32[]{:S(2)}) async-start(), calls=%async_computation.15 | async-start | bytes 2949120 | tf_op jit(solution)/shard_map/all_gather | solution.py:145
  399.0 170.6 %all-gather.13.cloned.1.call-start = ((), (), s32[]{:S(2)}) async-start(), calls=%async_computation.21 | async-start | bytes 5308416 | tf_op jit(solution)/shard_map/all_gather | solution.py:136
  399.6 232.7 %reduce-scatter.8.cloned.1.call-start = ((), (), s32[]{:S(2)}) async-start(), calls=%async_computation.18 | async-start | bytes 1474560 | tf_op jit(solution)/shard_map/reduce_scatter | solution.py:157
  405.9 15.5 %all-to-all-start.7 = ((bf16[256,4,288]{0,2,1:T(8,128)(2,1)}), bf16[256,4,288]{0,2,1:T(8,128)(2,1)S(1)}, u32[]{:S(2)}, u32[]{:S(2)}) async-start(bf16[256,4,288]{0,2,1:T(8,128)(2,1)} %bitcast.33), calls=%async_computation.9 | async-start | bytes 1179648 | tf_op jit(solution)/shard_map/all_to_all | solution.py:144
  421.3 44.1 %all-to-all-start.9 = ((bf16[256,4,1152]{2,0,1:T(8,128)(2,1)}), bf16[256,4,1152]{2,0,1:T(8,128)(2,1)S(1)}, u32[]{:S(2)}, u32[]{:S(2)}) async-start(bf16[256,4,1152]{2,0,1:T(8,128)(2,1)} %bitcast.164), calls=%async_computation.13 | async-start | bytes 4718592 | tf_op jit(solution)/shard_map/all_to_all | solution.py:144
  425.0 216.3 %reduce-scatter.10.cloned.1.call-start = ((), (), s32[]{:S(2)}) async-start(), calls=%async_computation.20 | async-start | bytes 995328 | tf_op jit(solution)/shard_map/reduce_scatter | solution.py:147
  430.7 225.3 %reduce-scatter.14.cloned.1.call-start = ((), (), s32[]{:S(2)}) async-start(), calls=%async_computation.23 | async-start | bytes 2985984 | tf_op jit(solution)/shard_map/reduce_scatter | solution.py:147
  474.4 18.1 %all-to-all-start.6 = ((bf16[256,4,576]{0,2,1:T(8,128)(2,1)}), bf16[256,4,576]{0,2,1:T(8,128)(2,1)S(1)}, u32[]{:S(2)}, u32[]{:S(2)}) async-start(bf16[256,4,576]{0,2,1:T(8,128)(2,1)} %pad_maximum_fusion), calls=%async_computation.6 | async-start | bytes 2359296 | tf_op jit(solution)/shard_map/all_to_all | solution.py:144
  493.5 74.3 %all-to-all-start.8 = ((bf16[256,8,576]{0,2,1:T(8,128)(2,1)}), bf16[256,8,576]{0,2,1:T(8,128)(2,1)S(1)}, u32[]{:S(2)}, u32[]{:S(2)}) async-start(bf16[256,8,576]{0,2,1:T(8,128)(2,1)} %bitcast.35), calls=%async_computation.11 | async-start | bytes 4718592 | tf_op jit(solution)/shard_map/all_to_all | solution.py:137
  498.0 183.5 %reduce-scatter.6.cloned.1.call-start = ((), (), s32[]{:S(2)}) async-start(), calls=%async_computation.16 | async-start | bytes 1658880 | tf_op jit(solution)/shard_map/reduce_scatter | solution.py:147
  505.8 207.2 %reduce-scatter.12.cloned.1.call-start = ((), (), s32[]{:S(2)}) async-start(), calls=%async_computation.22 | async-start | bytes 1843200 | tf_op jit(solution)/shard_map/reduce_scatter | solution.py:139
  577.9 48.5 %copy-start.22 = (bf16[256,1152]{1,0:T(8,128)(2,1)S(1)}, bf16[256,1152]{1,0:T(8,128)(2,1)}, u32[]{:S(2)}) copy-start(bf16[256,1152]{1,0:T(8,128)(2,1)} %get-tuple-element.284) | copy-start | bytes 1769476
  630.8 84.1 %copy-start.1 = (bf16[1152,1152]{1,0:T(8,128)(2,1)S(1)}, bf16[1152,1152]{1,0:T(8,128)(2,1)}, u32[]{:S(2)}) copy-start(bf16[1152,1152]{1,0:T(8,128)(2,1)} %param.29) | copy-start | bytes 7962628
  634.5 19.3 %collective-permute-start.2 = (f32[288,144]{1,0:T(8,128)}, f32[288,144]{1,0:T(8,128)}, u32[]{:S(2)}, u32[]{:S(2)}) collective-permute-start(f32[288,144]{1,0:T(8,128)} %get-tuple-element.301), channel_id=1, source_target_pairs={{0,8},{4,20},{8,0},{12,12},{16,24},{20,4},{24,16},{28,28},{1,9},{5... | collective-permute-start | bytes 497672 | tf_op jit(solution)/shard_map/ppermute | solution.py:168
  639.2 14.6 %collective-permute-start.1 = (f32[288,144]{1,0:T(8,128)S(1)}, f32[288,144]{1,0:T(8,128)}, u32[]{:S(2)}, u32[]{:S(2)}) collective-permute-start(f32[288,144]{1,0:T(8,128)S(1)} %get-tuple-element.302), channel_id=1, source_target_pairs={{0,20},{4,0},{8,12},{12,24},{16,4},{20,16},{24,28},{28,8},{1,21},{... | collective-permute-start | bytes 497672 | tf_op jit(solution)/shard_map/ppermute | solution.py:168
  639.3 14.5 %collective-permute-start = (f32[288,144]{1,0:T(8,128)S(1)}, f32[288,144]{1,0:T(8,128)}, u32[]{:S(2)}, u32[]{:S(2)}) collective-permute-start(f32[288,144]{1,0:T(8,128)S(1)} %get-tuple-element.300), channel_id=1, source_target_pairs={{0,0},{4,12},{8,24},{12,4},{16,16},{20,28},{24,8},{28,20},{1,1},{5... | collective-permute-start | bytes 497672 | tf_op jit(solution)/shard_map/ppermute | solution.py:168
  (54 other events, 257.8 us)
Sparse Core Ops, SparseCore 0:
  143.6 53.6 all-gather.8
  222.6 38.7 all-gather.10
  356.5 38.7 all-gather.14
  399.2 66.5 all-gather.6
  467.8 65.8 all-gather.12
  536.5 34.6 reduce-scatter.7
  573.5 32.1 reduce-scatter.9
  608.0 37.3 reduce-scatter.13
  647.7 33.7 reduce-scatter.5
  684.3 28.6 reduce-scatter.11
where the time goes:
time: 729 us; the launch traced here: 722 us
  waiting for transfers between devices  290 us (40%)
  matrix products  195 us (27%)
  local copies, waits for them, and re-layouts  64.7 us (9%)
  blocking collectives  58.1 us (8%)
  other arithmetic  52 us (7%)
  starting transfers between devices  46.1 us (6%)
  between operations  15.3 us (2%)
    all_to_all x1, waiting for transfers between devices, seq_gathered_grad(): lax.all_to_all(right, 'seq', split_axis=1, concat_axis=0, tiled=True)  61.5 us
    all_to_all x3, waiting for transfers between devices, batch_gathered_grad(): lax.all_to_all(left, 'batch', split_axis=1, concat_axis=0, tiled=True)  54.5 us
    all_to_all x1, waiting for transfers between devices, on_device(): lax.all_to_all(packed.reshape(local_rows, 3, seq_count, feature_count //...  41.7 us
    dot_general x5, matrix products, product(): return jnp.dot(left, right, preferred_element_type=jnp.float32)  40.6 us
    psum x1, blocking collectives, on_device(): small_total = lax.psum(jnp.concatenate(small_grads), ('seq', 'batch'))  38.9 us
    dot_general x5, matrix products, times_transposed(): lax.dot_general(left, right, (((1,), (1,)), ((), ())), preferred_element_...  37.2 us
    dot_general x5, matrix products, contract_rows(): lax.dot_general(left, right, (((0,), (0,)), ((), ())), preferred_element_...  30.8 us
    reduce_scatter x1, waiting for transfers between devices, seq_gathered_grad(): summed = lax.psum_scatter(partial, 'batch', scatter_dimension=0, tiled=True)  29.8 us
  transfers between devices with their start and end apart: 22, of which 12 were waited for; matrix products, arithmetic and copies ran while one was open for 31% of the time, Pallas kernels for 0%

commit v1 on v0

--- a/solution.py
+++ b/solution.py
@@ -289,7 +289,7 @@
         grad_down_bias,
     )
     small_sizes = [piece.shape[0] for piece in small_grads]
-    small_total = lax.psum(jnp.concatenate(small_grads), ("seq", "batch"))
+    small_total = jnp.sum(lax.all_gather(jnp.concatenate(small_grads), ("seq", "batch")), axis=0)
     summed_small = []
     offset = 0
     for size in small_sizes:

time: 729 us -> 783 us (1.074)
  waiting for transfers between devices: 290 us -> 370 us
  blocking collectives: 58.1 us -> 37.1 us
    psum x1 -> x0, blocking collectives: 38.9 us -> none  [on_device(): small_total = lax.psum(jnp.concatenate(small_grads), ('seq', 'batch'))]
    all_gather x0 -> x1, waiting for transfers between devices: none -> 31.8 us  [on_device(): lax.all_gather(jnp.concatenate(small_grads), ('seq', 'batch'))]
    reduce_scatter x3, waiting for transfers between devices: 23.6 us -> 52.2 us  [batch_gathered_grad(): summed = lax.psum_scatter(partial, 'seq', scatter_dimension=1, tiled=True)]
    reduce_scatter x1, waiting for transfers between devices: 0.01 us -> 27.5 us  [qkv_grad_from_heads(): summed = lax.psum_scatter(partial, 'batch', scatter_dimension=0, tiled=True)]
    all_to_all x3 -> x2, waiting for transfers between devices: 54.5 us -> 35.7 us  [batch_gathered_grad(): lax.all_to_all(left, 'batch', split_axis=1, concat_axis=0, tiled=True)]
    all_to_all x0 -> x1, blocking collectives: none -> 17.9 us  [batch_gathered_grad(): lax.all_to_all(left, 'batch', split_axis=1, concat_axis=0, tiled=True)]
    ppermute x3, waiting for transfers between devices: 10.9 us -> 21.3 us  [qkv_grad_from_heads(): slots.append(lax.ppermute(sent, 'seq', pairs))]
  transfers between devices with their start and end apart: 22 -> 22, of which waited for: 12 -> 15; matrix products, arithmetic and copies ran while one was open for 31% -> 23% of each run, Pallas kernels for 0% -> 0%
where the time goes in v1:
time: 783 us; the launch traced here: 777 us
  waiting for transfers between devices  370 us (47%)
  matrix products  194 us (25%)
  local copies, waits for them, and re-layouts  64.7 us (8%)
  other arithmetic  52.7 us (7%)
  starting transfers between devices  41.9 us (5%)
  blocking collectives  37.1 us (5%)
  between operations  15 us (2%)
    all_to_all x1, waiting for transfers between devices, seq_gathered_grad(): lax.all_to_all(right, 'seq', split_axis=1, concat_axis=0, tiled=True)  66.9 us
    reduce_scatter x3, waiting for transfers between devices, batch_gathered_grad(): summed = lax.psum_scatter(partial, 'seq', scatter_dimension=1, tiled=True)  52.2 us
    all_to_all x1, waiting for transfers between devices, on_device(): lax.all_to_all(packed.reshape(local_rows, 3, seq_count, feature_count //...  41.7 us
    dot_general x5, matrix products, product(): return jnp.dot(left, right, preferred_element_type=jnp.float32)  40.6 us
    dot_general x5, matrix products, times_transposed(): lax.dot_general(left, right, (((1,), (1,)), ((), ())), preferred_element_...  35.8 us
    all_to_all x2, waiting for transfers between devices, batch_gathered_grad(): lax.all_to_all(left, 'batch', split_axis=1, concat_axis=0, tiled=True)  35.7 us
    all_gather x1, waiting for transfers between devices, on_device(): lax.all_gather(jnp.concatenate(small_grads), ('seq', 'batch'))  31.8 us
    dot_general x5, matrix products, contract_rows(): lax.dot_general(left, right, (((0,), (0,)), ((), ())), preferred_element_...  31.2 us
  transfers between devices with their start and end apart: 22, of which 15 were waited for; matrix products, arithmetic and copies ran while one was open for 23% of the time, Pallas kernels for 0%

profile of v1, /device:TPU:0, one launch (start us, length us, event | category | flops | bytes accessed | tf_op | source)
XLA Modules:
  0.0 776.6 jit_solution(15446802588496685752)
XLA Ops:
  16.0 7.3 convolution_convert_fusion.1
  30.0 6.6 all-to-all-start
  36.9 41.7 %all-to-all-done = bf16[256,3,8,144]{0,3,1,2:T(8,128)(2,1)} async-done(((bf16[256,3,8,144]{0,3,1,2:T(8,128)(2,1)}), bf16[256,3,8,144]{0,3,1,2:T(8,128)(2,1)}, u32[]{:S(2)}, u32[]{:S(2)}) %all-to-all-start) | async-done | bytes 1769504 | tf_op jit(solution)/shard_map/all_to_all | solution.py:211
  93.9 36.5 %while.27 = (s32[]{:T(128)}, bf16[4,512,144]{1,2,0:T(8,128)(2,1)}, f32[4,2,512,1]{2,1,3,0:T(2,128)S(1)}, s32[4,512]{1,0:T(4,128)S(1)}, s32[2048]{0:T(1024)S(1)},...) while((s32[]{:T(128)}, bf16[4,512,144]{1,2,0:T(8,128)(2,1)}, ...), condition=%wide.region_7.8_spmd, body=%wide.region_4.7_spmd.sunk | while | flops 628169728 | bytes 33536144 | solution.py:74
  141.6 16.4 %all-to-all-done.1 = bf16[8,256,144]{1,2,0:T(8,128)(2,1)} async-done(((bf16[8,256,144]{1,2,0:T(8,128)(2,1)}), bf16[8,256,144]{1,2,0:T(8,128)(2,1)}, u32[]{:S(2)}, u32[]{:S(2)}) %all-to-all-start.1) | async-done | bytes 589856 | tf_op jit(solution)/shard_map/all_to_all | solution.py:223
  162.7 17.2 %multiply_convert_fusion.1 = (bf16[256,4608]{1,0:T(8,128)(2,1)}, f32[256,4608]{1,0:T(8,128)}, f32[256,4608]{1,0:T(8,128)}) fusion(f32[4608]{0:T(1024)S(1)} %convert_element_type.134, bf16[256,1152]{1,0:T(8,128)(2,1)} %add_convert_fusion.2, bf16[1152,4608]{1,0:T(8,128)(2,1)} %param.33), kind=kOutput, calls=%fused_computation.57 | convolution fusion | flops 2795765760 | bytes 23021568 | tf_op jit(solution)/shard_map/dot_general | solution.py:12
  179.9 14.0 %convert_reduce_fusion = (f32[4608]{0:T(1024)S(1)}, bf16[256,4608]{1,0:T(8,128)(2,1)}) fusion(f32[256,4608]{1,0:T(8,128)} %get-tuple-element.290, f32[256,4608]{1,0:T(8,128)} %get-tuple-element.315, bf16[4608,1152]{1,0:T(8,128)(2,1)} %param.35, bf16[1,256,1152]{2,1,0:T(8,128)(2,1)S(1)} %copy-done.14), kind=kOutput, calls=%fused_computation.55 | convolution fusion | flops 2736778752 | bytes 23021568 | tf_op jit(solution)/shard_map/dot_general | solution.py:22
  193.9 8.1 %multiply_reduce_fusion.1 = (f32[1152]{0:T(1024)S(1)}, f32[256]{0:T(256)S(1)}, f32[1152]{0:T(1024)S(1)}, f32[256,1152]{1,0:T(8,128)S(1)}) fusion(f32[256,1152]{1,0:T(8,128)S(1)} %copy-done.7, f32[256]{0:T(256)S(1)} %fusion.69, f32[256]{0:T(256)S(1)} %broadcast_multiply_fusion, f32[1152]{0:T(1024)S(1)} %convert_element_type.131, ...), kind=kOutput, calls=%fused_computation.106 | convolution fusion | flops 2720265728 | bytes 15352320 | tf_op jit(solution)/shard_map/dot_general | solution.py:22
  214.0 15.9 %all-to-all-done.2 = bf16[256,8,144]{0,2,1:T(8,128)(2,1)S(1)} async-done(((bf16[256,8,144]{0,2,1:T(8,128)(2,1)}), bf16[256,8,144]{0,2,1:T(8,128)(2,1)S(1)}, u32[]{:S(2)}, u32[]{:S(2)}) %all-to-all-start.2) | async-done | bytes 589856 | tf_op jit(solution)/shard_map/all_to_all | solution.py:249
  232.2 87.6 %while.28 = (s32[]{:T(128)}, f32[2048,2,72]{0,2,1:T(8,128)S(1)}, f32[2048,2,72]{0,2,1:T(8,128)}, bf16[4,512,144]{1,2,0:T(8,128)(2,1)}, bf16[4,512,2,72]{1,3,2,0:...) while((s32[]{:T(128)}, f32[2048,2,72]{0,2,1:T(8,128)S(1)}, ...), condition=%wide.region_14.15_spmd.clone, body=%wide.region_12.14_spmd.clone.sunk | while | flops 1543781376 | bytes 136800560 | solution.py:120
  246.8 5.4 fusion.146
  268.9 5.2 fusion.146
  312.6 5.2 fusion.146
  327.9 15.5 %all-to-all-done.5 = bf16[8,256,144]{1,2,0:T(8,128)(2,1)} async-done(((bf16[8,256,144]{1,2,0:T(8,128)(2,1)}), bf16[8,256,144]{1,2,0:T(8,128)(2,1)}, u32[]{:S(2)}, u32[]{:S(2)}) %all-to-all-start.5) | async-done | bytes 589856 | tf_op jit(solution)/shard_map/all_to_all | solution.py:259
  351.0 13.3 %all-to-all-done.4 = bf16[8,256,144]{1,2,0:T(8,128)(2,1)} async-done(((bf16[8,256,144]{1,2,0:T(8,128)(2,1)}), bf16[8,256,144]{1,2,0:T(8,128)(2,1)}, u32[]{:S(2)}, u32[]{:S(2)}) %all-to-all-start.4) | async-done | bytes 589856 | tf_op jit(solution)/shard_map/all_to_all | solution.py:258
  364.3 19.3 %all_to_all.180 = bf16[8,256,144]{1,2,0:T(8,128)(2,1)S(1)} all-to-all(bf16[8,256,144]{1,2,0:T(8,128)(2,1)S(1)} %copy.108), channel_id=1, replica_groups=mesh['seq'=8,'batch'=4] {'seq'}, dimensions={0} | all-to-all | bytes 1179648 | tf_op jit(solution)/shard_map/all_to_all | solution.py:257
  383.6 6.5 multiply_reduce_fusion.2
  393.4 17.9 %all_to_all.181 = bf16[256,4,288]{0,2,1:T(8,128)(2,1)S(1)} all-to-all(bf16[256,4,288]{0,2,1:T(8,128)(2,1)} %bitcast.33), channel_id=1, replica_groups=mesh['seq'=8,'batch'=4] {'batch'}, dimensions={1} | all-to-all | bytes 1179648 | tf_op jit(solution)/shard_map/all_to_all | solution.py:144
  423.9 6.1 convolution_convert_fusion.4
  430.3 25.6 %all-to-all-done.9 = bf16[256,4,1152]{2,0,1:T(8,128)(2,1)} async-done(((bf16[256,4,1152]{2,0,1:T(8,128)(2,1)}), bf16[256,4,1152]{2,0,1:T(8,128)(2,1)}, u32[]{:S(2)}, u32[]{:S(2)}) %all-to-all-start.9) | async-done | bytes 2359328 | tf_op jit(solution)/shard_map/all_to_all | solution.py:144
  455.9 7.2 convolution_convert_fusion
  473.4 10.1 %all-to-all-done.6 = bf16[256,4,576]{0,2,1:T(8,128)(2,1)S(1)} async-done(((bf16[256,4,576]{0,2,1:T(8,128)(2,1)}), bf16[256,4,576]{0,2,1:T(8,128)(2,1)S(1)}, u32[]{:S(2)}, u32[]{:S(2)}) %all-to-all-start.6) | async-done | bytes 1179680 | tf_op jit(solution)/shard_map/all_to_all | solution.py:144
  491.8 5.3 convolution_convert_fusion.3
  497.4 66.9 %all-to-all-done.8 = bf16[256,8,576]{0,2,1:T(8,128)(2,1)S(1)} async-done(((bf16[256,8,576]{0,2,1:T(8,128)(2,1)}), bf16[256,8,576]{0,2,1:T(8,128)(2,1)S(1)}, u32[]{:S(2)}, u32[]{:S(2)}) %all-to-all-start.8) | async-done | bytes 2359328 | tf_op jit(solution)/shard_map/all_to_all | solution.py:137
  565.9 8.2 %convolution_convert_fusion.2 = bf16[1152,576]{1,0:T(8,128)(2,1)} fusion(bf16[2048,1152]{1,0:T(8,128)(2,1)} %all-gather.16.cloned.1.call-done, bf16[2048,576]{0,1:T(8,128)(2,1)} %bitcast.218), kind=kOutput, calls=%fused_computation.71 | convolution fusion | flops 2718572544 | bytes 8404992 | tf_op jit(solution)/shard_map/dot_general | solution.py:16
  574.3 8.9 %fusion.47 = bf16[1,256,1152]{2,1,0:T(8,128)(2,1)} fusion(f32[256,1152]{1,0:T(8,128)S(1)} %copy-done.8, bf16[256,4608]{1,0:T(8,128)(2,1)} %get-tuple-element.289, bf16[4608,1152]{1,0:T(8,128)(2,1)} %param.35, f32[1152]{0:T(1024)S(1)} %convert_element_type.136), kind=kOutput, calls=%fused_computation.82 | convolution fusion | flops 2718793728 | bytes 14750208 | tf_op jit(solution)/shard_map/dot_general | solution.py:12
  590.6 31.8 %all-gather.20.cloned.1.call-done = f32[32,1,12672]{2,1,0:T(1,128)} async-done(((f32[1,1,12672]{2,1,0:T(1,128)}), f32[32,1,12672]{2,1,0:T(1,128)}) %all-gather.20.cloned.1.call-update) | async-done | bytes 1622032 | tf_op jit(solution)/shard_map/all_gather | solution.py:292
  625.6 27.5 %reduce-scatter.8.cloned.1.call-done = bf16[288,432]{1,0:T(8,128)(2,1)} async-done(((bf16[1152,432]{1,0:T(8,128)(2,1)}), bf16[288,432]{1,0:T(8,128)(2,1)}) %reduce-scatter.8.cloned.1.call-update) | async-done | bytes 248848 | tf_op jit(solution)/shard_map/reduce_scatter | solution.py:157
  659.6 16.3 %collective-permute-done.2 = f32[288,144]{1,0:T(8,128)S(1)} collective-permute-done((f32[288,144]{1,0:T(8,128)S(1)}, f32[288,144]{1,0:T(8,128)S(1)}, u32[]{:S(2)}, u32[]{:S(2)}) %collective-permute-start.2) | collective-permute-done | bytes 165920 | tf_op jit(solution)/shard_map/ppermute | solution.py:168
  682.0 18.9 %reduce-scatter.14.cloned.1.call-done = bf16[1152,144]{0,1:T(8,128)(2,1)} async-done(((bf16[1152,1152]{0,1:T(8,128)(2,1)}), bf16[1152,144]{0,1:T(8,128)(2,1)}) %reduce-scatter.14.cloned.1.call-update) | async-done | bytes 331792 | tf_op jit(solution)/shard_map/reduce_scatter | solution.py:147
  702.8 33.3 %reduce-scatter.6.cloned.1.call-done = bf16[576,144]{0,1:T(8,128)(2,1)} async-done(((bf16[576,1152]{0,1:T(8,128)(2,1)}), bf16[576,144]{0,1:T(8,128)(2,1)}) %reduce-scatter.6.cloned.1.call-update) | async-done | bytes 165904 | tf_op jit(solution)/shard_map/reduce_scatter | solution.py:147
  737.8 30.2 %reduce-scatter.12.cloned.1.call-done = bf16[288,576]{1,0:T(8,128)(2,1)} async-done(((bf16[1152,576]{1,0:T(8,128)(2,1)}), bf16[288,576]{1,0:T(8,128)(2,1)}) %reduce-scatter.12.cloned.1.call-update) | async-done | bytes 331792 | tf_op jit(solution)/shard_map/reduce_scatter | solution.py:139
  (315 shorter events, 249.5 us)
Async XLA Ops:
  7.2 150.8 %copy-start = (bf16[1152,1152]{1,0:T(8,128)(2,1)S(1)}, bf16[1152,1152]{1,0:T(8,128)(2,1)}, u32[]{:S(2)}) copy-start(bf16[1152,1152]{1,0:T(8,128)(2,1)} %param.29) | copy-start | bytes 7962628
  30.0 48.6 %all-to-all-start = ((bf16[256,3,8,144]{0,3,1,2:T(8,128)(2,1)}), bf16[256,3,8,144]{0,3,1,2:T(8,128)(2,1)}, u32[]{:S(2)}, u32[]{:S(2)}) async-start(bf16[256,3,8,144]{0,3,1,2:T(8,128)(2,1)} %copy.98), calls=%async_computation | async-start | bytes 3538944 | tf_op jit(solution)/shard_map/all_to_all | solution.py:211
  137.1 20.9 %all-to-all-start.1 = ((bf16[8,256,144]{1,2,0:T(8,128)(2,1)}), bf16[8,256,144]{1,2,0:T(8,128)(2,1)}, u32[]{:S(2)}, u32[]{:S(2)}) async-start(bf16[8,256,144]{1,2,0:T(8,128)(2,1)} %copy.102), calls=%async_computation.1 | async-start | bytes 1179648 | tf_op jit(solution)/shard_map/all_to_all | solution.py:223
  141.3 270.9 %all-gather.14.cloned.1.call-start = ((), (), s32[]{:S(2)}) async-start(), calls=%async_computation.19 | async-start | bytes 2949120 | tf_op jit(solution)/shard_map/all_gather | solution.py:145
  162.7 17.2 %copy-start.14 = (bf16[1,256,1152]{2,1,0:T(8,128)(2,1)S(1)}, bf16[1,256,1152]{2,1,0:T(8,128)(2,1)}, u32[]{:S(2)}) copy-start(bf16[1,256,1152]{2,1,0:T(8,128)(2,1)} %param.37) | copy-start | bytes 1769476
  179.9 14.0 %copy-start.7 = (f32[256,1152]{1,0:T(8,128)S(1)}, f32[256,1152]{1,0:T(8,128)}, u32[]{:S(2)}) copy-start(f32[256,1152]{1,0:T(8,128)} %copy-done.6) | copy-start | bytes 3538948
  209.6 20.2 %all-to-all-start.2 = ((bf16[256,8,144]{0,2,1:T(8,128)(2,1)}), bf16[256,8,144]{0,2,1:T(8,128)(2,1)S(1)}, u32[]{:S(2)}, u32[]{:S(2)}) async-start(bf16[256,8,144]{0,2,1:T(8,128)(2,1)} %bitcast.18), calls=%async_computation.2 | async-start | bytes 1179648 | tf_op jit(solution)/shard_map/all_to_all | solution.py:249
  213.2 210.6 %all-gather.12.cloned.1.call-start = ((), (), s32[]{:S(2)}) async-start(), calls=%async_computation.17 | async-start | bytes 5308416 | tf_op jit(solution)/shard_map/all_gather | solution.py:155
  322.3 26.1 %copy-start.13 = (bf16[4,512,144]{1,2,0:T(8,128)(2,1)S(1)}, bf16[4,512,144]{1,2,0:T(8,128)(2,1)}, u32[]{:S(2)}) copy-start(bf16[4,512,144]{1,2,0:T(8,128)(2,1)} %get-tuple-element.120) | copy-start | bytes 1769476
  322.3 21.1 %all-to-all-start.5 = ((bf16[8,256,144]{1,2,0:T(8,128)(2,1)}), bf16[8,256,144]{1,2,0:T(8,128)(2,1)}, u32[]{:S(2)}, u32[]{:S(2)}) async-start(bf16[8,256,144]{1,2,0:T(8,128)(2,1)} %copy.110), calls=%async_computation.5 | async-start | bytes 1179648 | tf_op jit(solution)/shard_map/all_to_all | solution.py:259
  326.8 24.2 %copy-start.19 = (bf16[2048,2,72]{0,2,1:T(8,128)(2,1)}, bf16[2048,2,72]{0,2,1:T(8,128)(2,1)S(1)}, u32[]{:S(2)}) copy-start(bf16[2048,2,72]{0,2,1:T(8,128)(2,1)S(1)} %multiply_convert_fusion.2) | copy-start | bytes 1769476
  327.8 55.8 %copy-start.10 = (f32[256,1152]{1,0:T(8,128)S(1)}, f32[256,1152]{1,0:T(8,128)}, u32[]{:S(2)}) copy-start(f32[256,1152]{1,0:T(8,128)} %copy-done.9) | copy-start | bytes 3538948
  327.8 55.8 %copy-start.29 = (f32[1152]{0:T(1024)S(1)}, f32[1152]{0:T(1024)}, u32[]{:S(2)}) copy-start(f32[1152]{0:T(1024)} %copy-done.28) | copy-start | bytes 13828
  327.8 55.8 %copy-start.31 = (f32[256]{0:T(256)S(1)}, f32[256]{0:T(256)}, u32[]{:S(2)}) copy-start(f32[256]{0:T(256)} %copy-done.30) | copy-start | bytes 3076
  327.8 55.8 %copy-start.36 = (f32[256]{0:T(256)S(1)}, f32[256]{0:T(256)}, u32[]{:S(2)}) copy-start(f32[256]{0:T(256)} %copy-done.35) | copy-start | bytes 3076
  343.4 20.9 %all-to-all-start.4 = ((bf16[8,256,144]{1,2,0:T(8,128)(2,1)}), bf16[8,256,144]{1,2,0:T(8,128)(2,1)}, u32[]{:S(2)}, u32[]{:S(2)}) async-start(bf16[8,256,144]{1,2,0:T(8,128)(2,1)} %copy.109), calls=%async_computation.4 | async-start | bytes 1179648 | tf_op jit(solution)/shard_map/all_to_all | solution.py:258
  347.6 82.7 %all-gather.18.cloned.1.call-start = ((), (), s32[]{:S(2)}) async-start(), calls=%async_computation.24 | async-start | bytes 2949120 | tf_op jit(solution)/shard_map/all_gather | solution.py:145
  348.3 143.4 %all-gather.10.cloned.1.call-start = ((), (), s32[]{:S(2)}) async-start(), calls=%async_computation.15 | async-start | bytes 2949120 | tf_op jit(solution)/shard_map/all_gather | solution.py:145
  392.7 173.2 %all-gather.16.cloned.1.call-start = ((), (), s32[]{:S(2)}) async-start(), calls=%async_computation.21 | async-start | bytes 5308416 | tf_op jit(solution)/shard_map/all_gather | solution.py:136
  393.3 195.7 %reduce-scatter.10.cloned.1.call-start = ((), (), s32[]{:S(2)}) async-start(), calls=%async_computation.20 | async-start | bytes 995328 | tf_op jit(solution)/shard_map/reduce_scatter | solution.py:147
  416.5 205.9 %all-gather.20.cloned.1.call-start = ((), (), s32[]{:S(2)}) async-start(), calls=%async_computation.25 | async-start | bytes 1672704 | tf_op jit(solution)/shard_map/all_gather | solution.py:292
  419.0 36.9 %all-to-all-start.9 = ((bf16[256,4,1152]{2,0,1:T(8,128)(2,1)}), bf16[256,4,1152]{2,0,1:T(8,128)(2,1)}, u32[]{:S(2)}, u32[]{:S(2)}) async-start(bf16[256,4,1152]{2,0,1:T(8,128)(2,1)} %bitcast.164), calls=%async_computation.13 | async-start | bytes 4718592 | tf_op jit(solution)/shard_map/all_to_all | solution.py:144
  423.7 229.4 %reduce-scatter.8.cloned.1.call-start = ((), (), s32[]{:S(2)}) async-start(), calls=%async_computation.18 | async-start | bytes 1474560 | tf_op jit(solution)/shard_map/reduce_scatter | solution.py:157
  430.0 270.9 %reduce-scatter.14.cloned.1.call-start = ((), (), s32[]{:S(2)}) async-start(), calls=%async_computation.23 | async-start | bytes 2985984 | tf_op jit(solution)/shard_map/reduce_scatter | solution.py:147
  465.6 17.9 %all-to-all-start.6 = ((bf16[256,4,576]{0,2,1:T(8,128)(2,1)}), bf16[256,4,576]{0,2,1:T(8,128)(2,1)S(1)}, u32[]{:S(2)}, u32[]{:S(2)}) async-start(bf16[256,4,576]{0,2,1:T(8,128)(2,1)} %pad_maximum_fusion), calls=%async_computation.6 | async-start | bytes 2359296 | tf_op jit(solution)/shard_map/all_to_all | solution.py:144
  484.5 79.7 %all-to-all-start.8 = ((bf16[256,8,576]{0,2,1:T(8,128)(2,1)}), bf16[256,8,576]{0,2,1:T(8,128)(2,1)S(1)}, u32[]{:S(2)}, u32[]{:S(2)}) async-start(bf16[256,8,576]{0,2,1:T(8,128)(2,1)} %bitcast.35), calls=%async_computation.11 | async-start | bytes 4718592 | tf_op jit(solution)/shard_map/all_to_all | solution.py:137
  489.3 246.8 %reduce-scatter.6.cloned.1.call-start = ((), (), s32[]{:S(2)}) async-start(), calls=%async_computation.16 | async-start | bytes 1658880 | tf_op jit(solution)/shard_map/reduce_scatter | solution.py:147
  497.1 270.8 %reduce-scatter.12.cloned.1.call-start = ((), (), s32[]{:S(2)}) async-start(), calls=%async_computation.22 | async-start | bytes 1843200 | tf_op jit(solution)/shard_map/reduce_scatter | solution.py:139
  622.5 147.4 %copy-start.1 = (bf16[1152,1152]{1,0:T(8,128)(2,1)S(1)}, bf16[1152,1152]{1,0:T(8,128)(2,1)}, u32[]{:S(2)}) copy-start(bf16[1152,1152]{1,0:T(8,128)(2,1)} %param.29) | copy-start | bytes 7962628
  654.4 21.5 %collective-permute-start.2 = (f32[288,144]{1,0:T(8,128)S(1)}, f32[288,144]{1,0:T(8,128)S(1)}, u32[]{:S(2)}, u32[]{:S(2)}) collective-permute-start(f32[288,144]{1,0:T(8,128)S(1)} %get-tuple-element.301), channel_id=1, source_target_pairs={{0,8},{4,20},{8,0},{12,12},{16,24},{20,4},{24,16},{28,28},{1,9},{5... | collective-permute-start | bytes 497672 | tf_op jit(solution)/shard_map/ppermute | solution.py:168
  657.8 23.1 %collective-permute-start.1 = (f32[288,144]{1,0:T(8,128)S(1)}, f32[288,144]{1,0:T(8,128)S(1)}, u32[]{:S(2)}, u32[]{:S(2)}) collective-permute-start(f32[288,144]{1,0:T(8,128)S(1)} %get-tuple-element.302), channel_id=1, source_target_pairs={{0,20},{4,0},{8,12},{12,24},{16,4},{20,16},{24,28},{28,8},{1,21},{... | collective-permute-start | bytes 497672 | tf_op jit(solution)/shard_map/ppermute | solution.py:168
  658.3 22.6 %collective-permute-start = (f32[288,144]{1,0:T(8,128)S(1)}, f32[288,144]{1,0:T(8,128)S(1)}, u32[]{:S(2)}, u32[]{:S(2)}) collective-permute-start(f32[288,144]{1,0:T(8,128)S(1)} %get-tuple-element.300), channel_id=1, source_target_pairs={{0,0},{4,12},{8,24},{12,4},{16,16},{20,28},{24,8},{28,20},{1,1},{5... | collective-permute-start | bytes 497672 | tf_op jit(solution)/shard_map/ppermute | solution.py:168
  (50 other events, 223.0 us)
Sparse Core Ops, SparseCore 0:
  204.7 36.2 all-gather.13
  242.6 51.1 all-gather.11
  350.2 38.5 all-gather.17
  392.9 57.7 all-gather.9
  452.7 65.3 all-gather.15
  520.2 42.9 reduce-scatter.9
  566.6 55.7 all-gather.19
  625.4 27.6 reduce-scatter.7
  655.4 45.4 reduce-scatter.13
  703.1 32.9 reduce-scatter.5
  739.0 28.8 reduce-scatter.11
